TPU v7x, 32 devices: a whole 2x2x4 slice. The times are simulated.
32 devices in a mesh: gx: 2 (over x), gy: 4 (over z), gz: 4 (over y, core).
Axes of the slice: x: 2, y: 2, z: 4, core: 2. Of those that a mesh axis runs over, the one named last changes fastest.
Arguments:
- acts: bfloat16 [40960, 768], P(('gx', 'gy', 'gz')), may hold values from -6 to 6
- grads_out: bfloat16 [40960, 768], P(('gx', 'gy', 'gz')), may hold values from -0.03125 to 0.03125
- master: float32 [4608, 128], P(('gx', 'gy', 'gz')), may hold values from -0.3 to 0.3
- moment: float32 [4608, 128], P(('gx', 'gy', 'gz')), may hold values from -6 to 6
- second: float32 [4608, 128], P(('gx', 'gy', 'gz')), may hold values from 0.1 to 2
Outputs:
- master_new: float32 [4608, 128], P(('gx', 'gy', 'gz'))
- moment_new: float32 [4608, 128], P(('gx', 'gy', 'gz'))
- second_new: float32 [4608, 128], P(('gx', 'gy', 'gz'))
- weights: bfloat16 [768, 768], replicated
All inputs are finite; a program needn't handle non-finite values.
Results may differ from a plain program's by a relative error of at most 0.003.
Values may be sent and summed in bfloat16 or wider, within the bound.
No kernel may reach another device: no remote copies, remote signals or barrier semaphores. Data moves between devices by JAX's collectives and lax.ppermute only.
A program may use at most 64 MiB of HBM per device.

v0:
```python
import jax
import jax.numpy as jnp
from jax import lax
from jax.sharding import PartitionSpec as P

STEP = 1000


def shards(acts, grads_out, master, moment, second):
    width_in = acts.shape[1]
    width_out = grads_out.shape[1]
    lane = master.shape[1]
    total_rows = width_in * width_out // lane
    local_grad = lax.dot_general(
        acts, grads_out, (((0,), (0,)), ((), ())), preferred_element_type=jnp.float32
    )
    local_flat = local_grad.reshape(total_rows, lane)
    partial_value = lax.psum_scatter(
        local_flat.astype(jnp.bfloat16), "gx", scatter_dimension=0, tiled=True
    ).astype(jnp.float32)
    partial_value = lax.psum_scatter(
        partial_value.astype(jnp.bfloat16), "gy", scatter_dimension=0, tiled=True
    ).astype(jnp.float32)
    gradient = lax.psum_scatter(
        partial_value.astype(jnp.bfloat16), "gz", scatter_dimension=0, tiled=True
    ).astype(jnp.float32)
    moment_new = 0.9 * moment + 0.1 * gradient
    second_new = 0.95 * second + 0.05 * gradient * gradient
    first_fix = 1.0 - 0.9**STEP
    second_fix = 1.0 - 0.95**STEP
    ratio = moment_new / first_fix / (jnp.sqrt(second_new / second_fix) + 1e-08)
    master_new = master - 0.01 * (ratio + 0.01 * master)
    rounded = master_new.astype(jnp.bfloat16)
    gathered = lax.all_gather(rounded, "gz", axis=0, tiled=True)
    gathered = lax.all_gather(gathered, "gy", axis=0, tiled=True)
    gathered = lax.all_gather(gathered, "gx", axis=0, tiled=True)
    weights = gathered.reshape(width_in, width_out)
    return (master_new, moment_new, second_new, weights)


def solution(mesh):
    return jax.shard_map(
        shards,
        mesh=mesh,
        in_specs=(
            P(("gx", "gy", "gz"), None),
            P(("gx", "gy", "gz"), None),
            P(("gx", "gy", "gz"), None),
            P(("gx", "gy", "gz"), None),
            P(("gx", "gy", "gz"), None),
        ),
        out_specs=(
            P(("gx", "gy", "gz"), None),
            P(("gx", "gy", "gz"), None),
            P(("gx", "gy", "gz"), None),
            P(),
        ),
        check_vma=False,
    )
```

profile of v0, /device:TPU:0, one launch (start us, length us, event | category | flops | bytes accessed | tf_op | source)
XLA Modules:
  0.0 141.0 jit_solution(13236243267090482629)
XLA Ops:
  7.2 0.0 copy-start
  7.2 0.0 reduce-scatter.4.cloned.1.call-start
  7.2 1.5 %copy-done = bf16[1280,768]{1,0:T(8,128)(2,1)S(1)} copy-done((bf16[1280,768]{1,0:T(8,128)(2,1)S(1)}, bf16[1280,768]{1,0:T(8,128)(2,1)}, u32[]{:S(2)}) %copy-start) | copy-done | bytes 1966104
  8.7 3.3 %convolution_convert_fusion = bf16[768,768]{1,0:T(8,128)(2,1)S(1)} fusion(bf16[1280,768]{1,0:T(8,128)(2,1)S(1)} %copy-done, bf16[1280,768]{1,0:T(8,128)(2,1)} %param.6), kind=kOutput, calls=%fused_computation | convolution fusion | flops 1510539264 | bytes 5111808 | tf_op jit(solution)/shard_map/dot_general | solution.py:14
  12.0 0.0 copy-start.1
  12.0 0.0 copy-start.2
  12.0 0.0 copy-start.3
  12.1 1.9 %convert_element_type.17 = bf16[4608,128]{1,0:T(8,128)(2,1)} reshape(bf16[768,768]{1,0:T(8,128)(2,1)S(1)} %convolution_convert_fusion) | data formatting | bytes 2359296 | tf_op jit(solution)/shard_map/convert_element_type | solution.py:19
  13.9 0.0 reduce-scatter.4.cloned.1.call-update
  13.9 0.0 reduce-scatter.6.cloned.1.call-start
  14.0 24.7 %reduce-scatter.4.cloned.1.call-done = bf16[2304,128]{1,0:T(8,128)(2,1)} async-done(((bf16[4608,128]{1,0:T(8,128)(2,1)}), bf16[2304,128]{1,0:T(8,128)(2,1)}) %reduce-scatter.4.cloned.1.call-update) | async-done | bytes 589840 | tf_op jit(solution)/shard_map/reduce_scatter | solution.py:18
  38.7 0.0 reduce-scatter.6.cloned.1.call-update
  38.7 0.0 reduce-scatter.8.cloned.1.call-start
  38.7 24.4 %reduce-scatter.6.cloned.1.call-done = bf16[576,128]{1,0:T(8,128)(2,1)} async-done(((bf16[2304,128]{1,0:T(8,128)(2,1)}), bf16[576,128]{1,0:T(8,128)(2,1)}) %reduce-scatter.6.cloned.1.call-update) | async-done | bytes 147472 | tf_op jit(solution)/shard_map/reduce_scatter | solution.py:21
  63.1 0.0 reduce-scatter.8.cloned.1.call-update
  63.1 0.0 all-gather.2.cloned.1.call-start
  63.2 20.5 %reduce-scatter.8.cloned.1.call-done = bf16[144,128]{1,0:T(8,128)(2,1)} async-done(((bf16[576,128]{1,0:T(8,128)(2,1)}), bf16[144,128]{1,0:T(8,128)(2,1)}) %reduce-scatter.8.cloned.1.call-update) | async-done | bytes 36880 | tf_op jit(solution)/shard_map/reduce_scatter | solution.py:24
  83.7 0.0 copy-done.1
  83.7 0.0 copy-done.2
  83.7 0.0 copy-done.3
  83.7 1.5 %fusion.2 = (bf16[144,128]{1,0:T(8,128)(2,1)S(1)}, f32[144,128]{1,0:T(8,128)}, f32[144,128]{1,0:T(8,128)}, f32[144,128]{1,0:T(8,128)}) fusion(f32[144,128]{1,0:T(8,128)S(1)} %copy-done.1, bf16[144,128]{1,0:T(8,128)(2,1)} %reduce-scatter.8.cloned.1.call-done, f32[144,128]{1,0:T(8,128)S(1)} %copy-done.2, f32[144,128]{1,0:T(8,128)S(1)} %copy-done.3), kind=kLoop, calls=%fused_computation.6 | loop fusion | flops 276480 | bytes 516096 | tf_op jit(solution)/shard_map/convert_element_type | solution.py:33
  85.2 5.4 %all_gather.9 = bf16[576,128]{1,0:T(8,128)(2,1)S(1)} all-gather(bf16[144,128]{1,0:T(8,128)(2,1)S(1)} %get-tuple-element.4), channel_id=1, replica_groups=mesh['gx'=2,'gy'=4,'gz'=4] {'gz'}, dimensions={0}, use_global_device_ids=true | all-gather | bytes 184320 | tf_op jit(solution)/shard_map/all_gather | solution.py:34
  90.6 17.2 %all_gather.10 = bf16[2304,128]{1,0:T(8,128)(2,1)} all-gather(bf16[576,128]{1,0:T(8,128)(2,1)S(1)} %all_gather.9), channel_id=1, replica_groups=mesh['gx'=2,'gy'=4,'gz'=4] {'gy'}, dimensions={0}, use_global_device_ids=true | all-gather | bytes 737280 | tf_op jit(solution)/shard_map/all_gather | solution.py:35
  107.8 0.0 all-gather.2.cloned.1.call-update
  107.8 23.3 %all-gather.2.cloned.1.call-done = bf16[4608,128]{1,0:T(8,128)(2,1)} async-done(((bf16[2304,128]{1,0:T(8,128)(2,1)}), bf16[4608,128]{1,0:T(8,128)(2,1)}) %all-gather.2.cloned.1.call-update) | async-done | bytes 1179664 | tf_op jit(solution)/shard_map/all_gather | solution.py:36
  131.1 3.3 %reshape.13 = bf16[768,768]{1,0:T(8,128)(2,1)} reshape(bf16[4608,128]{1,0:T(8,128)(2,1)} %all-gather.2.cloned.1.call-done) | data formatting | bytes 2359296 | tf_op jit(solution)/shard_map/reshape | solution.py:37
Async XLA Ops:
  7.2 1.6 %copy-start = (bf16[1280,768]{1,0:T(8,128)(2,1)S(1)}, bf16[1280,768]{1,0:T(8,128)(2,1)}, u32[]{:S(2)}) copy-start(bf16[1280,768]{1,0:T(8,128)(2,1)} %param.5) | copy-start | bytes 5898244
  7.2 31.5 %reduce-scatter.4.cloned.1.call-start = ((), (), s32[]{:S(2)}) async-start(), calls=%async_computation.3 | async-start | bytes 1769472 | tf_op jit(solution)/shard_map/reduce_scatter | solution.py:18
  12.0 71.7 %copy-start.1 = (f32[144,128]{1,0:T(8,128)S(1)}, f32[144,128]{1,0:T(8,128)}, u32[]{:S(2)}) copy-start(f32[144,128]{1,0:T(8,128)} %param.7) | copy-start | bytes 221188
  12.0 71.7 %copy-start.2 = (f32[144,128]{1,0:T(8,128)S(1)}, f32[144,128]{1,0:T(8,128)}, u32[]{:S(2)}) copy-start(f32[144,128]{1,0:T(8,128)} %param.9) | copy-start | bytes 221188
  12.0 71.7 %copy-start.3 = (f32[144,128]{1,0:T(8,128)S(1)}, f32[144,128]{1,0:T(8,128)}, u32[]{:S(2)}) copy-start(f32[144,128]{1,0:T(8,128)} %param.8) | copy-start | bytes 221188
  13.9 49.2 %reduce-scatter.6.cloned.1.call-start = ((), (), s32[]{:S(2)}) async-start(), calls=%async_computation.4 | async-start | bytes 737280 | tf_op jit(solution)/shard_map/reduce_scatter | solution.py:21
  38.7 45.0 %reduce-scatter.8.cloned.1.call-start = ((), (), s32[]{:S(2)}) async-start(), calls=%async_computation.5 | async-start | bytes 184320 | tf_op jit(solution)/shard_map/reduce_scatter | solution.py:24
  63.1 68.0 %all-gather.2.cloned.1.call-start = ((), (), s32[]{:S(2)}) async-start(), calls=%async_computation.6 | async-start | bytes 1769472 | tf_op jit(solution)/shard_map/all_gather | solution.py:36
Sparse Core Ops, SparseCore 0:
  14.1 24.5 reduce-scatter.3
  40.9 22.1 reduce-scatter.5
  65.5 18.1 reduce-scatter.7
  108.0 23.0 all-gather.1
where the time goes:
time: 141 us
  waiting for transfers between devices  92.9 us (66%)
  blocking collectives  22.6 us (16%)
  between operations  13.8 us (10%)
  local copies, waits for them, and re-layouts  6.73 us (5%)
  matrix products  3.29 us (2%)
  other arithmetic  1.48 us (1%)
    reduce_scatter x1, waiting for transfers between devices, shards(): lax.psum_scatter(local_flat.astype(jnp.bfloat16), 'gx', scatter_dimension...  24.7 us
    reduce_scatter x1, waiting for transfers between devices, shards(): lax.psum_scatter(partial_value.astype(jnp.bfloat16), 'gy', scatter_dimens...  24.4 us
    all_gather x1, waiting for transfers between devices, shards(): gathered = lax.all_gather(gathered, 'gx', axis=0, tiled=True)  23.3 us
    reduce_scatter x1, waiting for transfers between devices, shards(): lax.psum_scatter(partial_value.astype(jnp.bfloat16), 'gz', scatter_dimens...  20.5 us
    all_gather x1, blocking collectives, shards(): gathered = lax.all_gather(gathered, 'gy', axis=0, tiled=True)  17.2 us
    all_gather x1, blocking collectives, shards(): gathered = lax.all_gather(rounded, 'gz', axis=0, tiled=True)  5.45 us
    reshape x1, local copies, waits for them, and re-layouts, shards(): weights = gathered.reshape(width_in, width_out)  3.35 us
    dot_general x1, matrix products, shards(): lax.dot_general(acts, grads_out, (((0,), (0,)), ((), ())), preferred_elem...  3.29 us
  transfers between devices with their start and end apart: 4, of which 4 were waited for; matrix products, arithmetic and copies ran while one was open for 0% of the time, Pallas kernels for 0%

commit v1 on v0

--- a/solution.py
+++ b/solution.py
@@ -33,7 +33,9 @@
     rounded = master_new.astype(jnp.bfloat16)
     gathered = lax.all_gather(rounded, "gz", axis=0, tiled=True)
     gathered = lax.all_gather(gathered, "gy", axis=0, tiled=True)
-    gathered = lax.all_gather(gathered, "gx", axis=0, tiled=True)
+    gathered = jnp.concatenate(
+        lax.all_to_all(jnp.stack([gathered] * lax.axis_size("gx")), "gx", 0, 0), axis=0
+    )
     weights = gathered.reshape(width_in, width_out)
     return (master_new, moment_new, second_new, weights)
 

time: 141 us -> 133 us (0.943)
  waiting for transfers between devices: 92.9 us -> 69.7 us
  blocking collectives: 22.6 us -> 38.7 us
  local copies, waits for them, and re-layouts: 6.73 us -> 5.23 us
    all_gather x1 -> x0, waiting for transfers between devices: 23.3 us -> none  [shards(): gathered = lax.all_gather(gathered, 'gx', axis=0, tiled=True)]
    all_to_all x0 -> x1, blocking collectives: none -> 15.9 us  [shards(): lax.all_to_all(jnp.stack([gathered] * lax.axis_size('gx')), 'gx', 0, 0)]
    reshape x1 -> x0, local copies, waits for them, and re-layouts: 3.35 us -> none  [shards(): weights = gathered.reshape(width_in, width_out)]
    another operation x0 -> x1, local copies, waits for them, and re-layouts: none -> 1.85 us  [shards(): weights = gathered.reshape(width_in, width_out)]
  transfers between devices with their start and end apart: 4 -> 3, of which waited for: 4 -> 3; matrix products, arithmetic and copies ran while one was open for 0% -> 0% of each run, Pallas kernels for 0% -> 0%
where the time goes in v1:
time: 133 us; the launch traced here: 132 us
  waiting for transfers between devices  69.7 us (52%)
  blocking collectives  38.7 us (29%)
  between operations  13.8 us (10%)
  local copies, waits for them, and re-layouts  5.23 us (4%)
  matrix products  3.29 us (2%)
  other arithmetic  1.58 us (1%)
    reduce_scatter x1, waiting for transfers between devices, shards(): lax.psum_scatter(local_flat.astype(jnp.bfloat16), 'gx', scatter_dimension...  24.7 us
    reduce_scatter x1, waiting for transfers between devices, shards(): lax.psum_scatter(partial_value.astype(jnp.bfloat16), 'gy', scatter_dimens...  24.4 us
    reduce_scatter x1, waiting for transfers between devices, shards(): lax.psum_scatter(partial_value.astype(jnp.bfloat16), 'gz', scatter_dimens...  20.6 us
    all_gather x1, blocking collectives, shards(): gathered = lax.all_gather(gathered, 'gy', axis=0, tiled=True)  17.3 us
    all_to_all x1, blocking collectives, shards(): lax.all_to_all(jnp.stack([gathered] * lax.axis_size('gx')), 'gx', 0, 0)  15.9 us
    all_gather x1, blocking collectives, shards(): gathered = lax.all_gather(rounded, 'gz', axis=0, tiled=True)  5.45 us
    dot_general x1, matrix products, shards(): lax.dot_general(acts, grads_out, (((0,), (0,)), ((), ())), preferred_elem...  3.29 us
  transfers between devices with their start and end apart: 3, of which 3 were waited for; matrix products, arithmetic and copies ran while one was open for 0% of the time, Pallas kernels for 0%

profile of v1, /device:TPU:0, one launch (start us, length us, event | category | flops | bytes accessed | tf_op | source)
XLA Modules:
  0.0 132.3 jit_solution(4567253798917820112)
XLA Ops:
  7.2 0.0 copy-start
  7.2 0.0 reduce-scatter.4.cloned.1.call-start
  7.2 1.5 %copy-done = bf16[1280,768]{1,0:T(8,128)(2,1)S(1)} copy-done((bf16[1280,768]{1,0:T(8,128)(2,1)S(1)}, bf16[1280,768]{1,0:T(8,128)(2,1)}, u32[]{:S(2)}) %copy-start) | copy-done | bytes 1966104
  8.7 3.3 %convolution_convert_fusion = bf16[768,768]{1,0:T(8,128)(2,1)S(1)} fusion(bf16[1280,768]{1,0:T(8,128)(2,1)S(1)} %copy-done, bf16[1280,768]{1,0:T(8,128)(2,1)} %param.6), kind=kOutput, calls=%fused_computation | convolution fusion | flops 1510539264 | bytes 5111808 | tf_op jit(solution)/shard_map/dot_general | solution.py:14
  12.0 0.0 copy-start.1
  12.0 0.0 copy-start.2
  12.0 0.0 copy-start.3
  12.1 1.9 %convert_element_type.17 = bf16[4608,128]{1,0:T(8,128)(2,1)} reshape(bf16[768,768]{1,0:T(8,128)(2,1)S(1)} %convolution_convert_fusion) | data formatting | bytes 2359296 | tf_op jit(solution)/shard_map/convert_element_type | solution.py:19
  13.9 0.0 reduce-scatter.4.cloned.1.call-update
  13.9 0.0 reduce-scatter.6.cloned.1.call-start
  14.0 24.7 %reduce-scatter.4.cloned.1.call-done = bf16[2304,128]{1,0:T(8,128)(2,1)} async-done(((bf16[4608,128]{1,0:T(8,128)(2,1)}), bf16[2304,128]{1,0:T(8,128)(2,1)}) %reduce-scatter.4.cloned.1.call-update) | async-done | bytes 589840 | tf_op jit(solution)/shard_map/reduce_scatter | solution.py:18
  38.7 0.0 reduce-scatter.6.cloned.1.call-update
  38.7 0.0 reduce-scatter.8.cloned.1.call-start
  38.7 24.4 %reduce-scatter.6.cloned.1.call-done = bf16[576,128]{1,0:T(8,128)(2,1)} async-done(((bf16[2304,128]{1,0:T(8,128)(2,1)}), bf16[576,128]{1,0:T(8,128)(2,1)}) %reduce-scatter.6.cloned.1.call-update) | async-done | bytes 147472 | tf_op jit(solution)/shard_map/reduce_scatter | solution.py:21
  63.1 0.0 reduce-scatter.8.cloned.1.call-update
  63.1 20.6 %reduce-scatter.8.cloned.1.call-done = bf16[144,128]{1,0:T(8,128)(2,1)} async-done(((bf16[576,128]{1,0:T(8,128)(2,1)}), bf16[144,128]{1,0:T(8,128)(2,1)}) %reduce-scatter.8.cloned.1.call-update) | async-done | bytes 36880 | tf_op jit(solution)/shard_map/reduce_scatter | solution.py:24
  83.7 0.0 copy-done.1
  83.7 0.0 copy-done.2
  83.7 0.0 copy-done.3
  83.7 1.5 %fusion.2 = (bf16[144,128]{1,0:T(8,128)(2,1)S(1)}, f32[144,128]{1,0:T(8,128)}, f32[144,128]{1,0:T(8,128)}, f32[144,128]{1,0:T(8,128)}) fusion(f32[144,128]{1,0:T(8,128)S(1)} %copy-done.1, bf16[144,128]{1,0:T(8,128)(2,1)} %reduce-scatter.8.cloned.1.call-done, f32[144,128]{1,0:T(8,128)S(1)} %copy-done.2, f32[144,128]{1,0:T(8,128)S(1)} %copy-done.3), kind=kLoop, calls=%fused_computation.7 | loop fusion | flops 276480 | bytes 516096 | tf_op jit(solution)/shard_map/convert_element_type | solution.py:33
  85.2 5.4 %all_gather.6 = bf16[576,128]{1,0:T(8,128)(2,1)S(1)} all-gather(bf16[144,128]{1,0:T(8,128)(2,1)S(1)} %get-tuple-element.4), channel_id=1, replica_groups=mesh['gx'=2,'gy'=4,'gz'=4] {'gz'}, dimensions={0}, use_global_device_ids=true | all-gather | bytes 184320 | tf_op jit(solution)/shard_map/all_gather | solution.py:34
  90.6 17.3 %all_gather.7 = bf16[2304,128]{1,0:T(8,128)(2,1)S(1)} all-gather(bf16[576,128]{1,0:T(8,128)(2,1)S(1)} %all_gather.6), channel_id=1, replica_groups=mesh['gx'=2,'gy'=4,'gz'=4] {'gy'}, dimensions={0}, use_global_device_ids=true | all-gather | bytes 737280 | tf_op jit(solution)/shard_map/all_gather | solution.py:35
  107.9 0.1 pad_maximum_fusion
  108.0 15.9 %all_to_all.5 = bf16[2,2304,128]{2,1,0:T(8,128)(2,1)S(1)} all-to-all(bf16[2,2304,128]{2,1,0:T(8,128)(2,1)S(1)} %pad_maximum_fusion), channel_id=1, replica_groups=mesh['gx'=2,'gy'=4,'gz'=4] {'gx'}, dimensions={0} | all-to-all | bytes 2359296 | tf_op jit(solution)/shard_map/all_to_all | solution.py:37
  123.9 1.9 %reshape_reshape.3 = bf16[768,768]{1,0:T(8,128)(2,1)} reshape(bf16[2,2304,128]{2,1,0:T(8,128)(2,1)S(1)} %all_to_all.5) | data formatting | bytes 2359296 | tf_op jit(solution)/shard_map/reshape;reshape | solution.py:39
Async XLA Ops:
  7.2 1.6 %copy-start = (bf16[1280,768]{1,0:T(8,128)(2,1)S(1)}, bf16[1280,768]{1,0:T(8,128)(2,1)}, u32[]{:S(2)}) copy-start(bf16[1280,768]{1,0:T(8,128)(2,1)} %param.5) | copy-start | bytes 5898244
  7.2 31.5 %reduce-scatter.4.cloned.1.call-start = ((), (), s32[]{:S(2)}) async-start(), calls=%async_computation.4 | async-start | bytes 1769472 | tf_op jit(solution)/shard_map/reduce_scatter | solution.py:18
  12.0 71.7 %copy-start.1 = (f32[144,128]{1,0:T(8,128)S(1)}, f32[144,128]{1,0:T(8,128)}, u32[]{:S(2)}) copy-start(f32[144,128]{1,0:T(8,128)} %param.7) | copy-start | bytes 221188
  12.0 71.7 %copy-start.2 = (f32[144,128]{1,0:T(8,128)S(1)}, f32[144,128]{1,0:T(8,128)}, u32[]{:S(2)}) copy-start(f32[144,128]{1,0:T(8,128)} %param.9) | copy-start | bytes 221188
  12.0 71.7 %copy-start.3 = (f32[144,128]{1,0:T(8,128)S(1)}, f32[144,128]{1,0:T(8,128)}, u32[]{:S(2)}) copy-start(f32[144,128]{1,0:T(8,128)} %param.8) | copy-start | bytes 221188
  13.9 49.2 %reduce-scatter.6.cloned.1.call-start = ((), (), s32[]{:S(2)}) async-start(), calls=%async_computation.5 | async-start | bytes 737280 | tf_op jit(solution)/shard_map/reduce_scatter | solution.py:21
  38.7 45.0 %reduce-scatter.8.cloned.1.call-start = ((), (), s32[]{:S(2)}) async-start(), calls=%async_computation.6 | async-start | bytes 184320 | tf_op jit(solution)/shard_map/reduce_scatter | solution.py:24
Sparse Core Ops, SparseCore 0:
  14.1 24.5 reduce-scatter.3
  40.9 22.1 reduce-scatter.5
  65.5 18.1 reduce-scatter.7
